TPU v7x, 32 devices: a whole 2x2x4 slice. The times are simulated.
32 devices in a mesh: row: 8 (over z, core), col: 4 (over y, x).
Axes of the slice: x: 2, y: 2, z: 4, core: 2. Of those that a mesh axis runs over, the one named last changes fastest.
Arguments:
- tokens: bfloat16 [12288, 2048], P('row', 'col'), may hold values from -6 to 6
- weight_query: bfloat16 [2048, 2048], P('row', 'col'), may hold values from -0.125 to 0.125
- weight_key: bfloat16 [2048, 2048], P('row', 'col'), may hold values from -0.125 to 0.125
- weight_value: bfloat16 [2048, 2048], P('row', 'col'), may hold values from -0.125 to 0.125
- weight_output: bfloat16 [2048, 2048], P('col', 'row'), may hold values from -0.125 to 0.125
- weight_gate: bfloat16 [2048, 8192], P('row', 'col'), may hold values from -0.125 to 0.125
- weight_up: bfloat16 [2048, 8192], P('row', 'col'), may hold values from -0.125 to 0.125
- weight_down: bfloat16 [8192, 2048], P('col', 'row'), may hold values from -0.0625 to 0.0625
- gain_query: float32 [2048], P('col'), may hold values from 0.25 to 1.75
- gain_key: float32 [2048], P('col'), may hold values from 0.25 to 1.75
- gain_attention: float32 [2048], replicated, may hold values from 0.5 to 1.5
- gain_feedforward: float32 [2048], replicated, may hold values from 0.5 to 1.5
- positions: int32 [12288], P('row'), may hold values from 0 to 1279, as said below
- segments: int32 [12288], P('row'), may hold values from 0 to 2, as said below
- cotangent: bfloat16 [12288, 2048], P('row', 'col'), may hold values from -6 to 6
Outputs:
- activations: bfloat16 [12288, 2048], P('row', 'col')
- input_grad: float32 [12288, 2048], P('row', 'col')
- query_weight_grad: float32 [2048, 2048], P('row', 'col')
- key_weight_grad: float32 [2048, 2048], P('row', 'col')
- value_weight_grad: float32 [2048, 2048], P('row', 'col')
- output_weight_grad: float32 [2048, 2048], P('col', 'row')
- gate_weight_grad: float32 [2048, 8192], P('row', 'col')
- up_weight_grad: float32 [2048, 8192], P('row', 'col')
- down_weight_grad: float32 [8192, 2048], P('col', 'row')
- query_gain_grad: float32 [2048], P('col')
- key_gain_grad: float32 [2048], P('col')
- attention_gain_grad: float32 [2048], replicated
- feedforward_gain_grad: float32 [2048], replicated
Inputs may be any that keep to these rules, and one draw needn't show every extreme that they name: The 1536 rows of each index of row form one group: the prompt's 1024 rows are consecutive with segment 0 and positions 0 to 1023; each continuation has 256 consecutive rows, one segment of 1 to 2 (each once a group) and positions 1024 to 1279 in order; the prompt lies before, between or after whole continuations. `segments`: segment ids of the layout described for positions.
All inputs are finite; a program needn't handle non-finite values.
Results may differ from a plain program's by a relative error of at most 0.02.
Values may be sent and summed in bfloat16 or wider, within the bound.
A program may use at most 320 MiB of HBM per device.

v0:
```python
import jax
import jax.numpy as jnp
from jax import lax
from jax.sharding import PartitionSpec as P

D = 2048
HD = 128
EPSILON = 1e-06
ROPE_BASE = 500000.0
NEGATIVE = -1e30
block_limit = 512


def times_plain(left, right):
    return jnp.dot(left, right, preferred_element_type=jnp.float32)


def times_transposed(left, right):
    return lax.dot_general(
        left, right, (((1,), (1,)), ((), ())), preferred_element_type=jnp.float32
    )


def transposed_times(left, right):
    return lax.dot_general(
        left, right, (((0,), (0,)), ((), ())), preferred_element_type=jnp.float32
    )


def rotation(positions):
    half_dim = HD // 2
    inverse = ROPE_BASE ** (-(jnp.arange(half_dim).astype(jnp.float32) * 2.0) / HD)
    angles = positions.astype(jnp.float32)[:, None] * inverse[None, :]
    return (jnp.cos(angles), jnp.sin(angles))


def rotate(values, cosine_table, sine_table, direction):
    row_count, local_width = values.shape
    local_heads = local_width // HD
    half_dim = HD // 2
    shaped = values.reshape(row_count, local_heads, HD)
    lower_half = shaped[..., :half_dim]
    upper_half = shaped[..., half_dim:]
    cosine_rows = cosine_table[:, None, :]
    sine_rows = direction * sine_table[:, None, :]
    rotated = jnp.concatenate(
        [
            lower_half * cosine_rows - upper_half * sine_rows,
            upper_half * cosine_rows + lower_half * sine_rows,
        ],
        axis=-1,
    )
    return rotated.reshape(row_count, local_width)


def allowed_pairs(segment_block, position_block, segments, positions):
    shared = (segments[None, :] == 0) | (segments[None, :] == segment_block[:, None])
    return shared & (positions[None, :] <= position_block[:, None])


def norm_back(incoming, values, norm_scale, gain_vector):
    scaled = gain_vector * incoming
    inner_mean = jnp.mean(scaled * values, axis=-1, keepdims=True)
    grad_values = norm_scale * scaled - values * norm_scale * norm_scale * norm_scale * inner_mean
    return (grad_values, jnp.sum(incoming * values * norm_scale, axis=0))


def spread_share(values, start):
    return lax.dynamic_update_slice_in_dim(jnp.zeros((D,), jnp.float32), values, start, 0)


def attend(query_rot, key_rot, value_low, segments, positions):
    row_count, local_width = query_rot.shape
    local_heads = local_width // HD
    block_rows = min(block_limit, row_count)
    blocks = row_count // block_rows
    key_heads = key_rot.reshape(row_count, local_heads, HD)
    value_heads = value_low.reshape(row_count, local_heads, HD)

    def one_block(packed):
        query_block, segment_block, position_block = packed
        query_heads = query_block.reshape(block_rows, local_heads, HD)
        scores = jnp.einsum(
            "qhd,khd->hqk", query_heads, key_heads, preferred_element_type=jnp.float32
        ) * HD ** (-0.5)
        allowed = allowed_pairs(segment_block, position_block, segments, positions)
        scores = jnp.where(allowed[None], scores, NEGATIVE)
        row_max = jnp.max(scores, axis=-1, keepdims=True)
        exponent = jnp.exp(scores - row_max)
        row_total = jnp.sum(exponent, axis=-1, keepdims=True)
        attn_probs = exponent / row_total
        context = jnp.einsum(
            "hqk,khd->qhd",
            attn_probs.astype(jnp.bfloat16),
            value_heads,
            preferred_element_type=jnp.float32,
        )
        return (context.reshape(block_rows, local_width), (row_max + jnp.log(row_total))[..., 0])

    context, log_norm = lax.map(
        one_block,
        (
            query_rot.reshape(blocks, block_rows, local_width),
            segments.reshape(blocks, block_rows),
            positions.reshape(blocks, block_rows),
        ),
    )
    return (context.reshape(row_count, local_width), log_norm)


def attend_back(query_rot, key_rot, value_low, context_grad, log_norm, segments, positions):
    row_count, local_width = query_rot.shape
    local_heads = local_width // HD
    block_rows = min(block_limit, row_count)
    blocks = row_count // block_rows
    scale_factor = HD ** (-0.5)
    key_heads = key_rot.reshape(row_count, local_heads, HD)
    value_heads = value_low.reshape(row_count, local_heads, HD)

    def one_block(carry, packed):
        key_total, value_total = carry
        query_block, grad_block, norm_block, segment_block, position_block = packed
        query_heads = query_block.reshape(block_rows, local_heads, HD)
        grad_heads = grad_block.reshape(block_rows, local_heads, HD)
        scores = (
            jnp.einsum("qhd,khd->hqk", query_heads, key_heads, preferred_element_type=jnp.float32)
            * scale_factor
        )
        allowed = allowed_pairs(segment_block, position_block, segments, positions)
        scores = jnp.where(allowed[None], scores, NEGATIVE)
        attn_probs = jnp.exp(scores - norm_block[..., None])
        prob_grad = jnp.einsum(
            "qhd,khd->hqk", grad_heads, value_heads, preferred_element_type=jnp.float32
        )
        delta_sum = jnp.sum(attn_probs * prob_grad, axis=-1, keepdims=True)
        score_grad = (attn_probs * (prob_grad - delta_sum)).astype(jnp.bfloat16)
        query_grad = (
            jnp.einsum("hqk,khd->qhd", score_grad, key_heads, preferred_element_type=jnp.float32)
            * scale_factor
        )
        key_total = (
            key_total
            + jnp.einsum(
                "hqk,qhd->khd", score_grad, query_heads, preferred_element_type=jnp.float32
            )
            * scale_factor
        )
        value_total = value_total + jnp.einsum(
            "hqk,qhd->khd",
            attn_probs.astype(jnp.bfloat16),
            grad_heads,
            preferred_element_type=jnp.float32,
        )
        return ((key_total, value_total), query_grad.reshape(block_rows, local_width))

    zeros_heads = jnp.zeros((row_count, local_heads, HD), jnp.float32)
    packed = (
        query_rot.reshape(blocks, block_rows, local_width),
        context_grad.reshape(blocks, block_rows, local_width),
        log_norm,
        segments.reshape(blocks, block_rows),
        positions.reshape(blocks, block_rows),
    )
    (key_grad, value_grad), query_grad = lax.scan(one_block, (zeros_heads, zeros_heads), packed)
    return (
        query_grad.reshape(row_count, local_width),
        key_grad.reshape(row_count, local_width),
        value_grad.reshape(row_count, local_width),
    )


def body(
    tokens,
    weight_query,
    weight_key,
    weight_value,
    weight_output,
    weight_gate,
    weight_up,
    weight_down,
    gain_query,
    gain_key,
    gain_attention,
    gain_feedforward,
    positions,
    segments,
    cotangent,
):
    col_width = tokens.shape[1]
    col_start = lax.axis_index("col") * col_width
    features = lax.all_gather(tokens, "col", axis=1, tiled=True)
    query_matrix, key_matrix, value_matrix, output_matrix, gate_matrix, up_matrix, down_matrix = (
        lax.all_gather(weight_query, "row", axis=0, tiled=True),
        lax.all_gather(weight_key, "row", axis=0, tiled=True),
        lax.all_gather(weight_value, "row", axis=0, tiled=True),
        lax.all_gather(weight_output, "row", axis=1, tiled=True),
        lax.all_gather(weight_gate, "row", axis=0, tiled=True),
        lax.all_gather(weight_up, "row", axis=0, tiled=True),
        lax.all_gather(weight_down, "row", axis=1, tiled=True),
    )
    query_raw = times_plain(features, query_matrix)
    key_raw = times_plain(features, key_matrix)
    value_low = times_plain(features, value_matrix).astype(jnp.bfloat16)
    square_sums = lax.psum(
        (jnp.sum(query_raw * query_raw, axis=-1), jnp.sum(key_raw * key_raw, axis=-1)), "col"
    )
    query_scale = lax.rsqrt(square_sums[0] / D + EPSILON)[:, None]
    key_scale = lax.rsqrt(square_sums[1] / D + EPSILON)[:, None]
    cosine_table, sine_table = rotation(positions)
    query_rot = rotate(query_raw * query_scale * gain_query, cosine_table, sine_table, 1.0).astype(
        jnp.bfloat16
    )
    key_rot = rotate(key_raw * key_scale * gain_key, cosine_table, sine_table, 1.0).astype(
        jnp.bfloat16
    )
    context, log_norm = attend(query_rot, key_rot, value_low, segments, positions)
    context_low = context.astype(jnp.bfloat16)
    attention_part = times_plain(context_low, output_matrix)
    attention_out = lax.psum(attention_part, "col")
    attention_scale = lax.rsqrt(
        jnp.mean(attention_out * attention_out, axis=-1, keepdims=True) + EPSILON
    )
    hidden_state = features.astype(jnp.float32) + attention_out * attention_scale * gain_attention
    hidden_low = hidden_state.astype(jnp.bfloat16)
    gate = times_plain(hidden_low, gate_matrix)
    up_rows = times_plain(hidden_low, up_matrix)
    sigmoid_gate = jax.nn.sigmoid(gate)
    silu_gate = gate * sigmoid_gate
    activated = (silu_gate * up_rows).astype(jnp.bfloat16)
    feedforward_part = times_plain(activated, down_matrix)
    feedforward_out = lax.psum(feedforward_part, "col")
    feedforward_scale = lax.rsqrt(
        jnp.mean(feedforward_out * feedforward_out, axis=-1, keepdims=True) + EPSILON
    )
    result = hidden_state + feedforward_out * feedforward_scale * gain_feedforward
    activations = lax.dynamic_slice_in_dim(result, col_start, col_width, 1).astype(jnp.bfloat16)
    upstream = lax.all_gather(cotangent, "col", axis=1, tiled=True).astype(jnp.float32)
    feedforward_full_grad, feedforward_gain_full = norm_back(
        upstream, feedforward_out, feedforward_scale, gain_feedforward
    )
    feedforward_gain_part = lax.dynamic_slice_in_dim(feedforward_gain_full, col_start, col_width, 0)
    feedforward_grad = feedforward_full_grad.astype(jnp.bfloat16)
    activated_grad = times_transposed(feedforward_grad, down_matrix)
    down_weight_grad = transposed_times(activated, feedforward_grad)
    gate_grad = (
        activated_grad * up_rows * sigmoid_gate * (1.0 + gate * (1.0 - sigmoid_gate))
    ).astype(jnp.bfloat16)
    up_grad = (activated_grad * silu_gate).astype(jnp.bfloat16)
    hidden_part = times_transposed(gate_grad, gate_matrix) + times_transposed(up_grad, up_matrix)
    gate_weight_grad = transposed_times(hidden_low, gate_grad)
    up_weight_grad = transposed_times(hidden_low, up_grad)
    hidden_grad = lax.psum(hidden_part, "col") + upstream
    attention_full_grad, attention_gain_full = norm_back(
        hidden_grad, attention_out, attention_scale, gain_attention
    )
    attention_gain_part = lax.dynamic_slice_in_dim(attention_gain_full, col_start, col_width, 0)
    attention_grad = attention_full_grad.astype(jnp.bfloat16)
    residual_grad = lax.dynamic_slice_in_dim(hidden_grad, col_start, col_width, 1)
    context_grad = times_transposed(attention_grad, output_matrix).astype(jnp.bfloat16)
    output_weight_grad = transposed_times(context_low, attention_grad)
    query_rot_grad, key_rot_grad, value_grad = attend_back(
        query_rot, key_rot, value_low, context_grad, log_norm, segments, positions
    )
    value_grad = value_grad.astype(jnp.bfloat16)
    query_norm_grad = rotate(query_rot_grad, cosine_table, sine_table, -1.0)
    key_norm_grad = rotate(key_rot_grad, cosine_table, sine_table, -1.0)
    query_scaled = gain_query * query_norm_grad
    key_scaled = gain_key * key_norm_grad
    inner_sums = lax.psum(
        (jnp.sum(query_scaled * query_raw, axis=-1), jnp.sum(key_scaled * key_raw, axis=-1)), "col"
    )
    query_raw_grad = (
        query_scale * query_scaled
        - query_raw * query_scale * query_scale * query_scale * (inner_sums[0] / D)[:, None]
    ).astype(jnp.bfloat16)
    key_raw_grad = (
        key_scale * key_scaled
        - key_raw * key_scale * key_scale * key_scale * (inner_sums[1] / D)[:, None]
    ).astype(jnp.bfloat16)
    query_gain_part = jnp.sum(query_norm_grad * query_raw * query_scale, axis=0)
    key_gain_part = jnp.sum(key_norm_grad * key_raw * key_scale, axis=0)
    input_part = (
        times_transposed(query_raw_grad, query_matrix)
        + times_transposed(key_raw_grad, key_matrix)
        + times_transposed(value_grad, value_matrix)
    )
    query_weight_part = transposed_times(features, query_raw_grad)
    key_weight_part = transposed_times(features, key_raw_grad)
    value_weight_part = transposed_times(features, value_grad)
    input_grad = (
        lax.psum_scatter(
            input_part.astype(jnp.bfloat16), "col", scatter_dimension=1, tiled=True
        ).astype(jnp.float32)
        + residual_grad
    )
    weight_grads = (
        lax.psum_scatter(
            query_weight_part.astype(jnp.bfloat16), "row", scatter_dimension=0, tiled=True
        ).astype(jnp.float32),
        lax.psum_scatter(
            key_weight_part.astype(jnp.bfloat16), "row", scatter_dimension=0, tiled=True
        ).astype(jnp.float32),
        lax.psum_scatter(
            value_weight_part.astype(jnp.bfloat16), "row", scatter_dimension=0, tiled=True
        ).astype(jnp.float32),
        lax.psum_scatter(
            output_weight_grad.astype(jnp.bfloat16), "row", scatter_dimension=1, tiled=True
        ).astype(jnp.float32),
        lax.psum_scatter(
            gate_weight_grad.astype(jnp.bfloat16), "row", scatter_dimension=0, tiled=True
        ).astype(jnp.float32),
        lax.psum_scatter(
            up_weight_grad.astype(jnp.bfloat16), "row", scatter_dimension=0, tiled=True
        ).astype(jnp.float32),
        lax.psum_scatter(
            down_weight_grad.astype(jnp.bfloat16), "row", scatter_dimension=1, tiled=True
        ).astype(jnp.float32),
    )
    gain_totals = lax.psum(
        (
            spread_share(query_gain_part, col_start),
            spread_share(key_gain_part, col_start),
            spread_share(attention_gain_part, col_start),
            spread_share(feedforward_gain_part, col_start),
        ),
        ("row", "col"),
    )
    query_gain_grad = lax.dynamic_slice_in_dim(gain_totals[0], col_start, col_width, 0)
    key_gain_grad = lax.dynamic_slice_in_dim(gain_totals[1], col_start, col_width, 0)
    return (
        activations,
        input_grad,
        weight_grads[0],
        weight_grads[1],
        weight_grads[2],
        weight_grads[3],
        weight_grads[4],
        weight_grads[5],
        weight_grads[6],
        query_gain_grad,
        key_gain_grad,
        gain_totals[2],
        gain_totals[3],
    )


def solution(mesh):
    in_specs = (
        P("row", "col"),
        P("row", "col"),
        P("row", "col"),
        P("row", "col"),
        P("col", "row"),
        P("row", "col"),
        P("row", "col"),
        P("col", "row"),
        P("col"),
        P("col"),
        P(),
        P(),
        P("row"),
        P("row"),
        P("row", "col"),
    )
    out_specs = (
        P("row", "col"),
        P("row", "col"),
        P("row", "col"),
        P("row", "col"),
        P("row", "col"),
        P("col", "row"),
        P("row", "col"),
        P("row", "col"),
        P("col", "row"),
        P("col"),
        P("col"),
        P(),
        P(),
    )
    return jax.shard_map(body, mesh=mesh, in_specs=in_specs, out_specs=out_specs, check_vma=False)
```

profile of v0, /device:TPU:0, one launch (start us, length us, event | category | flops | bytes accessed | tf_op | source)
XLA Modules:
  0.0 2133.4 jit_solution(11342082336165431979)
XLA Ops:
  17.7 23.7 %all-gather.12.cloned.1.call-done = bf16[2048,512]{1,0:T(8,128)(2,1)} async-done(((bf16[256,512]{1,0:T(8,128)(2,1)}), bf16[2048,512]{1,0:T(8,128)(2,1)}) %all-gather.12.cloned.1.call-update) | async-done | bytes 2097168 | tf_op jit(solution)/shard_map/all_gather | solution.py:193
  41.5 71.2 %all-gather.10.cloned.1.call-done = bf16[1536,2048]{1,0:T(8,128)(2,1)} async-done(((bf16[1536,512]{1,0:T(8,128)(2,1)}), bf16[1536,2048]{1,0:T(8,128)(2,1)}) %all-gather.10.cloned.1.call-update) | async-done | bytes 6291472 | tf_op jit(solution)/shard_map/all_gather | solution.py:191
  112.7 6.3 multiply_reduce_fusion.8
  119.0 24.5 %all-gather.14.cloned.1.call-done = bf16[2048,512]{1,0:T(8,128)(2,1)} async-done(((bf16[256,512]{1,0:T(8,128)(2,1)}), bf16[2048,512]{1,0:T(8,128)(2,1)}) %all-gather.14.cloned.1.call-update) | async-done | bytes 2097168 | tf_op jit(solution)/shard_map/all_gather | solution.py:194
  143.4 8.6 multiply_reduce_fusion.7
  152.0 16.2 all-reduce.2
  186.1 6.2 subtract_convert_fusion.3
  203.0 8.1 convolution_convert_fusion.8
  211.1 47.7 %while.29 = (s32[]{:T(128)}, bf16[3,512,512]{2,1,0:T(8,128)(2,1)}, f32[3,4,512]{2,1,0:T(4,128)}, s32[1536]{0:T(1024)S(1)}, s32[3,512]{1,0:T(4,128)S(1)}, /*index...) while((s32[]{:T(128)}, bf16[3,512,512]{2,1,0:T(8,128)(2,1)}, ...), condition=%wide.region_7.8_spmd.clone, body=%wide.region_4.7_spmd.sunk.clone | while | flops 1651506688 | bytes 54626440 | solution.py:100
  221.0 5.1 fusion.138
  236.9 5.1 fusion.138
  252.7 5.1 fusion.138
  258.9 10.1 fusion.35
  271.3 234.8 %all-reduce.7.cloned.1.call-done = f32[1536,2048]{1,0:T(8,128)} async-done(((f32[1536,2048]{1,0:T(8,128)}), f32[1536,2048]{1,0:T(8,128)}) %all-reduce.7.cloned.1.call-update) | async-done | bytes 12582928 | tf_op jit(solution)/shard_map/psum | solution.py:219
  506.1 5.6 multiply_reduce_fusion.4
  514.3 10.6 fusion.31
  524.9 64.8 %all-gather.20.cloned.1.call-done = bf16[2048,2048]{1,0:T(8,128)(2,1)} async-done(((bf16[256,2048]{1,0:T(8,128)(2,1)}), bf16[2048,2048]{1,0:T(8,128)(2,1)}) %all-gather.20.cloned.1.call-update) | async-done | bytes 8388624 | tf_op jit(solution)/shard_map/all_gather | solution.py:197
  589.8 19.0 fusion.36
  608.7 63.2 %all-gather.22.cloned.1.call-done = bf16[2048,2048]{1,0:T(8,128)(2,1)} async-done(((bf16[256,2048]{1,0:T(8,128)(2,1)}), bf16[2048,2048]{1,0:T(8,128)(2,1)}) %all-gather.22.cloned.1.call-update) | async-done | bytes 8388624 | tf_op jit(solution)/shard_map/all_gather | solution.py:198
  671.9 23.5 %multiply_convert_fusion.3 = (bf16[1536,2048]{1,0:T(8,128)(2,1)}, f32[1536,2048]{1,0:T(8,128)}) fusion(f32[1536,2048]{1,0:T(8,128)} %fusion.36, bf16[1536,2048]{1,0:T(8,128)(2,1)} %get-tuple-element.317, bf16[2048,2048]{1,0:T(8,128)(2,1)} %all-gather.22.cloned.1.call-done), kind=kOutput, calls=%fused_computation.51 | convolution fusion | flops 12903776256 | bytes 46137344 | tf_op jit(solution)/shard_map/dot_general | solution.py:15
  695.5 59.0 %all-gather.24.cloned.1.call-done = bf16[2048,2048]{1,0:T(8,128)(2,1)} async-done(((bf16[2048,256]{1,0:T(8,128)(2,1)}), bf16[2048,2048]{1,0:T(8,128)(2,1)}) %all-gather.24.cloned.1.call-update) | async-done | bytes 8388624 | tf_op jit(solution)/shard_map/all_gather | solution.py:199
  754.5 18.9 fusion.37
  774.4 236.7 %all-reduce.9.cloned.1.call-done = f32[1536,2048]{1,0:T(8,128)} async-done(((f32[1536,2048]{1,0:T(8,128)}), f32[1536,2048]{1,0:T(8,128)}) %all-reduce.9.cloned.1.call-update) | async-done | bytes 12582928 | tf_op jit(solution)/shard_map/psum | solution.py:231
  1011.1 5.5 multiply_reduce_fusion.3
  1016.5 66.3 %all-gather.26.cloned.1.call-done = bf16[1536,2048]{1,0:T(8,128)(2,1)} async-done(((bf16[1536,512]{1,0:T(8,128)(2,1)}), bf16[1536,2048]{1,0:T(8,128)(2,1)}) %all-gather.26.cloned.1.call-update) | async-done | bytes 6291472 | tf_op jit(solution)/shard_map/all_gather | solution.py:237
  1082.8 10.2 fusion.21
  1094.6 7.9 fusion.18
  1102.5 26.6 %multiply_convert_fusion.1 = (bf16[1536,2048]{1,0:T(8,128)(2,1)}, bf16[1536,2048]{1,0:T(8,128)(2,1)}) fusion(f32[1536,2048]{1,0:T(8,128)} %fusion.36, f32[1536,2048]{1,0:T(8,128)} %get-tuple-element.355, bf16[1536,2048]{1,0:T(8,128)(2,1)} %get-tuple-element.329, bf16[2048,2048]{1,0:T(8,128)(2,1)} %all-gather.24.cloned.1.call-done), kind=kOutput, calls=%fused_computation.48 | convolution fusion | flops 12925796352 | bytes 52428800 | tf_op jit(solution)/shard_map/dot_general | solution.py:19
  1129.2 19.2 fusion.38
  1148.4 20.7 convolution_add_fusion
  1173.6 234.9 %all-reduce.11.cloned.1.call-done = f32[1536,2048]{1,0:T(8,128)} async-done(((f32[1536,2048]{1,0:T(8,128)}), f32[1536,2048]{1,0:T(8,128)}) %all-reduce.11.cloned.1.call-update) | async-done | bytes 12582928 | tf_op jit(solution)/shard_map/psum | solution.py:252
  1408.5 12.4 multiply_reduce_fusion.1
  1421.0 10.6 subtract_convert_fusion
  1436.2 127.1 %while.30 = (s32[]{:T(128)}, f32[1536,4,128]{0,2,1:T(8,128)}, f32[1536,4,128]{0,2,1:T(8,128)}, f32[3,512,512]{2,1,0:T(8,128)}, bf16[3,512,512]{1,2,0:T(8,128)(2,...) while((s32[]{:T(128)}, f32[1536,4,128]{0,2,1:T(8,128)}, ...), condition=%wide.region_17.18_spmd.clone.clone, body=%wide.region_15.17_spmd.clone.sunk.clone | while | flops 4062182912 | bytes 245442384 | solution.py:164
  1445.0 6.2 multiply_reduce_fusion.11
  1457.9 5.9 convolution_multiply_fusion.4
  1466.5 5.7 fusion.150
  1485.3 6.2 multiply_reduce_fusion.11
  1498.2 5.9 convolution_multiply_fusion.4
  1506.8 6.6 fusion.150
  1515.2 5.0 fusion.151
  1528.5 6.2 multiply_reduce_fusion.11
  1541.3 5.9 convolution_multiply_fusion.4
  1549.9 6.6 fusion.150
  1571.4 9.6 multiply_subtract_fusion
  1584.0 5.0 copy.57
  1595.8 5.2 copy.54
  1603.6 15.1 all-reduce.1
  1623.5 7.6 fusion.29
  1631.1 19.6 convolution_convert_fusion
  1650.8 8.2 convolution_convert_fusion.3
  1662.9 7.6 fusion.28
  1670.6 20.3 convolution_convert_fusion.2
  1691.0 20.0 convolution_convert_fusion.1
  1714.2 7.6 fusion.30
  1721.9 8.4 fusion.40
  1730.4 6.5 fusion.39
  1736.9 13.3 add_convert_fusion
  1758.0 41.1 %all-reduce = (f32[2048]{0:T(1024)S(1)}, f32[2048]{0:T(1024)S(1)}, f32[2048]{0:T(1024)}, f32[2048]{0:T(1024)}) all-reduce(f32[2048]{0:T(1024)S(1)} %dynamic_update_slice.23, f32[2048]{0:T(1024)S(1)} %dynamic_update_slice.24, f32[2048]{0:T(1024)S(1)} %dynamic-slice_dynamic-update-slice_fusion.1, ...), channel_id=1, replica_groups=mesh['row'=8,'col'=4] {'row','col'}, use_global_device_ids=true, to_apply=%region_31.32 | all-reduce | flops 8192 | bytes 65536 | tf_op jit(solution)/shard_map/psum | solution.py:319
  1806.8 25.9 %reduce-scatter.11.cloned.1.call-done = bf16[256,512]{0,1:T(8,128)(2,1)} async-done(((bf16[2048,512]{0,1:T(8,128)(2,1)}), bf16[256,512]{0,1:T(8,128)(2,1)}) %reduce-scatter.11.cloned.1.call-update) | async-done | bytes 262160 | tf_op jit(solution)/shard_map/reduce_scatter | solution.py:297
  1834.5 88.3 %reduce-scatter.19.cloned.1.call-done = bf16[256,2048]{1,0:T(8,128)(2,1)} async-done(((bf16[2048,2048]{1,0:T(8,128)(2,1)}), bf16[256,2048]{1,0:T(8,128)(2,1)}) %reduce-scatter.19.cloned.1.call-update) | async-done | bytes 1048592 | tf_op jit(solution)/shard_map/reduce_scatter | solution.py:309
  1925.6 87.4 %reduce-scatter.21.cloned.1.call-done = bf16[256,2048]{1,0:T(8,128)(2,1)} async-done(((bf16[2048,2048]{1,0:T(8,128)(2,1)}), bf16[256,2048]{1,0:T(8,128)(2,1)}) %reduce-scatter.21.cloned.1.call-update) | async-done | bytes 1048592 | tf_op jit(solution)/shard_map/reduce_scatter | solution.py:312
  2015.8 34.6 %reduce-scatter.15.cloned.1.call-done = bf16[256,512]{0,1:T(8,128)(2,1)} async-done(((bf16[2048,512]{0,1:T(8,128)(2,1)}), bf16[256,512]{0,1:T(8,128)(2,1)}) %reduce-scatter.15.cloned.1.call-update) | async-done | bytes 262160 | tf_op jit(solution)/shard_map/reduce_scatter | solution.py:303
  2052.3 69.5 %reduce-scatter.9.cloned.1.call-done = bf16[1536,512]{1,0:T(8,128)(2,1)} async-done(((bf16[1536,2048]{1,0:T(8,128)(2,1)}), bf16[1536,512]{1,0:T(8,128)(2,1)}) %reduce-scatter.9.cloned.1.call-update) | async-done | bytes 1572880 | tf_op jit(solution)/shard_map/reduce_scatter | solution.py:291
  (301 shorter events, 215.8 us)
Async XLA Ops:
  7.2 6.1 copy-start.23
  7.2 34.3 %all-gather.12.cloned.1.call-start = ((), (), s32[]{:S(2)}) async-start(), calls=%async_computation.9 | async-start | bytes 2359296 | tf_op jit(solution)/shard_map/all_gather | solution.py:193
  7.9 104.7 %all-gather.10.cloned.1.call-start = ((), (), s32[]{:S(2)}) async-start(), calls=%async_computation.8 | async-start | bytes 7864320 | tf_op jit(solution)/shard_map/all_gather | solution.py:191
  8.7 134.8 %all-gather.14.cloned.1.call-start = ((), (), s32[]{:S(2)}) async-start(), calls=%async_computation.10 | async-start | bytes 2359296 | tf_op jit(solution)/shard_map/all_gather | solution.py:194
  9.4 193.6 %all-gather.16.cloned.1.call-start = ((), (), s32[]{:S(2)}) async-start(), calls=%async_computation.11 | async-start | bytes 2359296 | tf_op jit(solution)/shard_map/all_gather | solution.py:195
  10.0 248.9 %all-gather.18.cloned.1.call-start = ((), (), s32[]{:S(2)}) async-start(), calls=%async_computation.12 | async-start | bytes 2359296 | tf_op jit(solution)/shard_map/all_gather | solution.py:196
  10.6 495.5 %all-reduce.7.cloned.1.call-start = ((), (), s32[]{:S(2)}) async-start(), calls=%async_computation.13 | async-start | bytes 25165824 | tf_op jit(solution)/shard_map/psum | solution.py:219
  119.0 49.3 %copy-start.11 = (f32[1536,512]{0,1:T(8,128)}, f32[1536,512]{0,1:T(8,128)S(1)}, u32[]{:S(2)}) copy-start(f32[1536,512]{0,1:T(8,128)S(1)} %get-tuple-element.351) | copy-start | bytes 9437188
  119.0 49.3 %copy-start.47 = (f32[512]{0:T(512)S(1)}, f32[512]{0:T(512)}, u32[]{:S(2)}) copy-start(f32[512]{0:T(512)} %param.27) | copy-start | bytes 6148
  168.3 9.0 copy-start.36
  203.0 8.1 copy-start.32
  258.9 10.1 copy-start.40
  258.9 10.1 copy-start.41
  269.0 320.8 %all-gather.20.cloned.1.call-start = ((), (), s32[]{:S(2)}) async-start(), calls=%async_computation.14 | async-start | bytes 9437184 | tf_op jit(solution)/shard_map/all_gather | solution.py:197
  269.7 402.2 %all-gather.22.cloned.1.call-start = ((), (), s32[]{:S(2)}) async-start(), calls=%async_computation.15 | async-start | bytes 9437184 | tf_op jit(solution)/shard_map/all_gather | solution.py:198
  270.5 484.0 %all-gather.24.cloned.1.call-start = ((), (), s32[]{:S(2)}) async-start(), calls=%async_computation.16 | async-start | bytes 9437184 | tf_op jit(solution)/shard_map/all_gather | solution.py:199
  271.2 241.1 %copy-start.42 = (f32[2048]{0:T(1024)S(1)}, f32[2048]{0:T(1024)}, u32[]{:S(2)}) copy-start(f32[2048]{0:T(1024)} %param.29) | copy-start | bytes 24580
  271.2 739.8 %all-reduce.9.cloned.1.call-start = ((), (), s32[]{:S(2)}) async-start(), calls=%async_computation.17 | async-start | bytes 25165824 | tf_op jit(solution)/shard_map/psum | solution.py:231
  506.1 8.2 copy-start.2
  773.4 309.4 %all-gather.26.cloned.1.call-start = ((), (), s32[]{:S(2)}) async-start(), calls=%async_computation.18 | async-start | bytes 7864320 | tf_op jit(solution)/shard_map/all_gather | solution.py:237
  774.2 308.6 %copy-start.44 = (f32[2048]{0:T(1024)S(1)}, f32[2048]{0:T(1024)}, u32[]{:S(2)}) copy-start(f32[2048]{0:T(1024)} %param.30) | copy-start | bytes 24580
  774.2 634.3 %all-reduce.11.cloned.1.call-start = ((), (), s32[]{:S(2)}) async-start(), calls=%async_computation.19 | async-start | bytes 25165824 | tf_op jit(solution)/shard_map/psum | solution.py:252
  1082.8 10.2 copy-start.6
  1082.8 11.8 copy-start.10
  1129.2 19.2 copy-start.51
  1169.1 631.3 %reduce-scatter.13.cloned.1.call-start = ((), (), s32[]{:S(2)}) async-start(), calls=%async_computation.22 | async-start | bytes 2359296 | tf_op jit(solution)/shard_map/reduce_scatter | solution.py:300
  1170.5 238.1 %copy-start.39 = (f32[1536]{0:T(1024)S(1)}, f32[1536]{0:T(1024)}, u32[]{:S(2)}) copy-start(f32[1536]{0:T(1024)} %copy-done.38) | copy-start | bytes 18436
  1170.5 238.1 %copy-start.43 = (f32[2048]{0:T(1024)S(1)}, f32[2048]{0:T(1024)}, u32[]{:S(2)}) copy-start(f32[2048]{0:T(1024)} %param.29) | copy-start | bytes 24580
  1421.0 10.6 copy-start.8
  1421.0 10.6 copy-start.50
  1431.6 4.6 copy-start.22
  1431.6 4.6 copy-start.24
  1436.7 5.8 copy-start.4
  1451.2 6.6 copy-start
  1451.2 6.6 copy-start.9
  1466.5 7.5 copy-start.1
  1477.0 5.7 copy-start.4
  1491.5 6.6 copy-start
  1491.5 6.6 copy-start.9
  1506.8 8.4 copy-start.1
  1515.2 5.0 copy-start.5
  1520.2 5.7 copy-start.4
  1534.7 6.6 copy-start
  1534.7 6.6 copy-start.9
  1549.9 8.4 copy-start.1
  1558.3 5.0 copy-start.5
  1584.0 5.1 copy-start.14
  1584.0 5.1 copy-start.37
  1584.0 5.1 copy-start.46
  1595.8 5.2 copy-start.12
  1595.8 5.2 copy-start.35
  1595.8 5.2 copy-start.48
  1631.1 171.2 %reduce-scatter.23.cloned.1.call-start = ((), (), s32[]{:S(2)}) async-start(), calls=%async_computation.27 | async-start | bytes 9437184 | tf_op jit(solution)/shard_map/reduce_scatter | solution.py:315
  1650.8 154.2 %reduce-scatter.17.cloned.1.call-start = ((), (), s32[]{:S(2)}) async-start(), calls=%async_computation.24 | async-start | bytes 2359296 | tf_op jit(solution)/shard_map/reduce_scatter | solution.py:306
  1659.0 173.6 %reduce-scatter.11.cloned.1.call-start = ((), (), s32[]{:S(2)}) async-start(), calls=%async_computation.21 | async-start | bytes 2359296 | tf_op jit(solution)/shard_map/reduce_scatter | solution.py:297
  1670.6 252.3 %reduce-scatter.19.cloned.1.call-start = ((), (), s32[]{:S(2)}) async-start(), calls=%async_computation.25 | async-start | bytes 9437184 | tf_op jit(solution)/shard_map/reduce_scatter | solution.py:309
  1691.0 322.0 %reduce-scatter.21.cloned.1.call-start = ((), (), s32[]{:S(2)}) async-start(), calls=%async_computation.26 | async-start | bytes 9437184 | tf_op jit(solution)/shard_map/reduce_scatter | solution.py:312
  1711.0 339.4 %reduce-scatter.15.cloned.1.call-start = ((), (), s32[]{:S(2)}) async-start(), calls=%async_computation.23 | async-start | bytes 2359296 | tf_op jit(solution)/shard_map/reduce_scatter | solution.py:303
  1714.2 7.6 copy-start.29
  1721.8 400.0 %reduce-scatter.9.cloned.1.call-start = ((), (), s32[]{:S(2)}) async-start(), calls=%async_computation.20 | async-start | bytes 7864320 | tf_op jit(solution)/shard_map/reduce_scatter | solution.py:291
  1721.9 8.5 copy-start.31
  1721.9 8.4 copy-start.49
  1730.4 6.6 copy-start.21
  1730.4 6.6 copy-start.25
  (22 other events, 60.8 us)
Sparse Core Ops, SparseCore 0:
  9.6 31.8 all-gather.11
  43.3 69.3 all-gather.9
  114.3 29.1 all-gather.13
  144.9 28.5 all-gather.15
  174.9 30.0 all-gather.17
  269.1 236.9 all-reduce.6
  507.7 82.0 all-gather.19
  591.4 80.5 all-gather.21
  673.5 80.9 all-gather.23
  773.6 237.4 all-reduce.8
  1012.9 69.8 all-gather.25
  1169.2 239.2 all-reduce.10
  1631.2 36.1 reduce-scatter.12
  1669.5 87.8 reduce-scatter.22
  1760.1 34.8 reduce-scatter.16
  1797.7 34.8 reduce-scatter.10
  1834.8 88.0 reduce-scatter.18
  1925.0 87.9 reduce-scatter.20
  2015.9 34.5 reduce-scatter.14
  2053.3 68.5 reduce-scatter.8
where the time goes:
time: 2140 us; the launch traced here: 2130 us
  waiting for transfers between devices  1390 us (65%)
  matrix products  384 us (18%)
  other arithmetic  160 us (7%)
  local copies, waits for them, and re-layouts  109 us (5%)
  blocking collectives  72.4 us (3%)
    psum x1, waiting for transfers between devices, body(): feedforward_out = lax.psum(feedforward_part, 'col')  237 us
    psum x1, waiting for transfers between devices, body(): hidden_grad = lax.psum(hidden_part, 'col') + upstream  235 us
    psum x1, waiting for transfers between devices, body(): attention_out = lax.psum(attention_part, 'col')  235 us
    dot_general x7, matrix products, times_transposed(): lax.dot_general(left, right, (((1,), (1,)), ((), ())), preferred_element_...  99.4 us
    dot_general x7, matrix products, times_plain(): return jnp.dot(left, right, preferred_element_type=jnp.float32)  94.4 us
    dot_general x7, matrix products, transposed_times(): lax.dot_general(left, right, (((0,), (0,)), ((), ())), preferred_element_...  90.8 us
    reduce_scatter x1, waiting for transfers between devices, body(): lax.psum_scatter(gate_weight_grad.astype(jnp.bfloat16), 'row', scatter_di...  88.3 us
    reduce_scatter x1, waiting for transfers between devices, body(): lax.psum_scatter(up_weight_grad.astype(jnp.bfloat16), 'row', scatter_dime...  87.4 us
  transfers between devices with their start and end apart: 20, of which 15 were waited for; matrix products, arithmetic and copies ran while one was open for 15% of the time, Pallas kernels for 0%

commit v1 on v0

--- a/solution.py
+++ b/solution.py
@@ -9,6 +9,19 @@
 ROPE_BASE = 500000.0
 NEGATIVE = -1e30
 block_limit = 512
+
+
+def ring_gather(shard, axis, dim):
+    ways = lax.axis_size(axis)
+    up = [(d, (d + 1) % ways) for d in range(ways)]
+    down = [(d, (d - 1) % ways) for d in range(ways)]
+    earlier, later = ([shard], [shard])
+    for _ in range(ways // 2):
+        earlier.append(lax.ppermute(earlier[-1], axis, up))
+    for _ in range((ways - 1) // 2):
+        later.append(lax.ppermute(later[-1], axis, down))
+    line = jnp.concatenate([*earlier[::-1], *later[1:]], axis=dim)
+    return jnp.roll(line, (lax.axis_index(axis) - ways // 2) * shard.shape[dim], axis=dim)
 
 
 def times_plain(left, right):
@@ -188,7 +201,7 @@
 ):
     col_width = tokens.shape[1]
     col_start = lax.axis_index("col") * col_width
-    features = lax.all_gather(tokens, "col", axis=1, tiled=True)
+    features = ring_gather(tokens, "col", 1)
     query_matrix, key_matrix, value_matrix, output_matrix, gate_matrix, up_matrix, down_matrix = (
         lax.all_gather(weight_query, "row", axis=0, tiled=True),
         lax.all_gather(weight_key, "row", axis=0, tiled=True),

time: 2140 us -> 2130 us (level)
  waiting for transfers between devices: 1390 us -> 1360 us
    ppermute x0 -> x3, waiting for transfers between devices: none -> 89.5 us  [the longest x2 63 us: ring_gather(): earlier.append(lax.ppermute(earlier[-1], axis, up))]
    reduce_scatter x1, waiting for transfers between devices: 0.01 us -> 87.4 us  [body(): lax.psum_scatter(down_weight_grad.astype(jnp.bfloat16), 'row', scatter_di...]
    all_gather x1 -> x0, waiting for transfers between devices: 71.2 us -> none  [body(): features = lax.all_gather(tokens, 'col', axis=1, tiled=True)]
    reduce_scatter x1, waiting for transfers between devices: 34.6 us -> 0.01 us  [body(): lax.psum_scatter(value_weight_part.astype(jnp.bfloat16), 'row', scatter_d...]
    reduce_scatter x1, waiting for transfers between devices: 25.9 us -> 0.01 us  [body(): lax.psum_scatter(query_weight_part.astype(jnp.bfloat16), 'row', scatter_d...]
    all_gather x1, waiting for transfers between devices: 24.5 us -> 0.01 us  [body(): lax.all_gather(weight_key, 'row', axis=0, tiled=True)]
    reduce_scatter x1, waiting for transfers between devices: 88.3 us -> 64.3 us  [body(): lax.psum_scatter(gate_weight_grad.astype(jnp.bfloat16), 'row', scatter_di...]
    all_gather x1, waiting for transfers between devices: 23.7 us -> 0.02 us  [body(): lax.all_gather(weight_query, 'row', axis=0, tiled=True)]
  transfers between devices with their start and end apart: 20 -> 22, of which waited for: 15 -> 14; matrix products, arithmetic and copies ran while one was open for 15% -> 16% of each run, Pallas kernels for 0% -> 0%
where the time goes in v1:
time: 2130 us; the launch traced here: 2120 us
  waiting for transfers between devices  1360 us (64%)
  matrix products  375 us (18%)
  other arithmetic  169 us (8%)
  local copies, waits for them, and re-layouts  118 us (6%)
  blocking collectives  69.8 us (3%)
    psum x1, waiting for transfers between devices, body(): attention_out = lax.psum(attention_part, 'col')  238 us
    psum x1, waiting for transfers between devices, body(): feedforward_out = lax.psum(feedforward_part, 'col')  237 us
    psum x1, waiting for transfers between devices, body(): hidden_grad = lax.psum(hidden_part, 'col') + upstream  235 us
    dot_general x7, matrix products, times_transposed(): lax.dot_general(left, right, (((1,), (1,)), ((), ())), preferred_element_...  99.1 us
    dot_general x7, matrix products, times_plain(): return jnp.dot(left, right, preferred_element_type=jnp.float32)  95.6 us
    dot_general x7, matrix products, transposed_times(): lax.dot_general(left, right, (((0,), (0,)), ((), ())), preferred_element_...  90 us
    reduce_scatter x1, waiting for transfers between devices, body(): lax.psum_scatter(down_weight_grad.astype(jnp.bfloat16), 'row', scatter_di...  87.4 us
    reduce_scatter x1, waiting for transfers between devices, body(): lax.psum_scatter(up_weight_grad.astype(jnp.bfloat16), 'row', scatter_dime...  87.4 us
  transfers between devices with their start and end apart: 22, of which 14 were waited for; matrix products, arithmetic and copies ran while one was open for 16% of the time, Pallas kernels for 0%

profile of v1, /device:TPU:0, one launch (start us, length us, event | category | flops | bytes accessed | tf_op | source)
XLA Modules:
  0.0 2119.6 jit_solution(6939797391300652439)
XLA Ops:
  12.5 35.6 %collective-permute-done = bf16[1536,512]{1,0:T(8,128)(2,1)S(1)} collective-permute-done((bf16[1536,512]{1,0:T(8,128)(2,1)}, bf16[1536,512]{1,0:T(8,128)(2,1)S(1)}, u32[]{:S(2)}, u32[]{:S(2)}) %collective-permute-start) | collective-permute-done | bytes 1572896 | tf_op jit(solution)/shard_map/ppermute | solution.py:20
  58.8 27.5 %collective-permute-done.1 = bf16[1536,512]{1,0:T(8,128)(2,1)} collective-permute-done((bf16[1536,512]{1,0:T(8,128)(2,1)S(1)}, bf16[1536,512]{1,0:T(8,128)(2,1)}, u32[]{:S(2)}, u32[]{:S(2)}) %collective-permute-start.1) | collective-permute-done | bytes 1572896 | tf_op jit(solution)/shard_map/ppermute | solution.py:20
  91.7 26.5 %collective-permute-done.2 = bf16[1536,512]{1,0:T(8,128)(2,1)S(1)} collective-permute-done((bf16[1536,512]{1,0:T(8,128)(2,1)}, bf16[1536,512]{1,0:T(8,128)(2,1)S(1)}, u32[]{:S(2)}, u32[]{:S(2)}) %collective-permute-start.2) | collective-permute-done | bytes 1572896 | tf_op jit(solution)/shard_map/ppermute | solution.py:22
  126.1 6.3 multiply_reduce_fusion.7
  132.5 9.7 multiply_reduce_fusion.8
  142.2 14.5 all-reduce.2
  174.5 7.9 subtract_convert_fusion.3
  195.4 8.0 convolution_convert_fusion.8
  203.5 47.8 %while.29 = (s32[]{:T(128)}, bf16[3,512,512]{2,1,0:T(8,128)(2,1)}, f32[3,4,512]{2,1,0:T(4,128)}, s32[1536]{0:T(1024)S(1)}, s32[3,512]{1,0:T(4,128)S(1)}, /*index...) while((s32[]{:T(128)}, bf16[3,512,512]{2,1,0:T(8,128)(2,1)}, ...), condition=%wide.region_7.8_spmd.clone, body=%wide.region_4.7_spmd.sunk.clone | while | flops 1651506688 | bytes 54625432 | solution.py:113
  212.8 5.1 fusion.143
  228.7 5.1 fusion.143
  244.5 5.1 fusion.143
  251.3 10.1 fusion.46
  263.6 237.6 %all-reduce.7.cloned.1.call-done = f32[1536,2048]{1,0:T(8,128)} async-done(((f32[1536,2048]{1,0:T(8,128)}), f32[1536,2048]{1,0:T(8,128)}) %all-reduce.7.cloned.1.call-update) | async-done | bytes 12582928 | tf_op jit(solution)/shard_map/psum | solution.py:232
  501.2 5.6 multiply_reduce_fusion.4
  509.5 10.4 fusion.42
  519.9 64.8 %all-gather.17.cloned.1.call-done = bf16[2048,2048]{1,0:T(8,128)(2,1)} async-done(((bf16[256,2048]{1,0:T(8,128)(2,1)}), bf16[2048,2048]{1,0:T(8,128)(2,1)}) %all-gather.17.cloned.1.call-update) | async-done | bytes 8388624 | tf_op jit(solution)/shard_map/all_gather | solution.py:210
  584.7 18.9 fusion.47
  603.6 63.3 %all-gather.19.cloned.1.call-done = bf16[2048,2048]{1,0:T(8,128)(2,1)} async-done(((bf16[256,2048]{1,0:T(8,128)(2,1)}), bf16[2048,2048]{1,0:T(8,128)(2,1)}) %all-gather.19.cloned.1.call-update) | async-done | bytes 8388624 | tf_op jit(solution)/shard_map/all_gather | solution.py:211
  666.9 23.7 %multiply_convert_fusion.3 = (bf16[1536,2048]{1,0:T(8,128)(2,1)}, f32[1536,2048]{1,0:T(8,128)}) fusion(f32[1536,2048]{1,0:T(8,128)} %fusion.47, bf16[1536,2048]{1,0:T(8,128)(2,1)} %get-tuple-element.291, bf16[2048,2048]{1,0:T(8,128)(2,1)} %all-gather.19.cloned.1.call-done), kind=kOutput, calls=%fused_computation.51 | convolution fusion | flops 12903776256 | bytes 46137344 | tf_op jit(solution)/shard_map/dot_general | solution.py:28
  690.6 58.9 %all-gather.21.cloned.1.call-done = bf16[2048,2048]{1,0:T(8,128)(2,1)} async-done(((bf16[2048,256]{1,0:T(8,128)(2,1)}), bf16[2048,2048]{1,0:T(8,128)(2,1)}) %all-gather.21.cloned.1.call-update) | async-done | bytes 8388624 | tf_op jit(solution)/shard_map/all_gather | solution.py:212
  749.5 18.9 fusion.48
  769.2 236.8 %all-reduce.9.cloned.1.call-done = f32[1536,2048]{1,0:T(8,128)} async-done(((f32[1536,2048]{1,0:T(8,128)}), f32[1536,2048]{1,0:T(8,128)}) %all-reduce.9.cloned.1.call-update) | async-done | bytes 12582928 | tf_op jit(solution)/shard_map/psum | solution.py:244
  1006.0 5.5 multiply_reduce_fusion.3
  1011.5 66.1 %all-gather.23.cloned.1.call-done = bf16[1536,2048]{1,0:T(8,128)(2,1)} async-done(((bf16[1536,512]{1,0:T(8,128)(2,1)}), bf16[1536,2048]{1,0:T(8,128)(2,1)}) %all-gather.23.cloned.1.call-update) | async-done | bytes 6291472 | tf_op jit(solution)/shard_map/all_gather | solution.py:250
  1077.6 10.3 fusion.21
  1089.5 8.0 fusion.18
  1097.5 26.5 %multiply_convert_fusion.1 = (bf16[1536,2048]{1,0:T(8,128)(2,1)}, bf16[1536,2048]{1,0:T(8,128)(2,1)}) fusion(f32[1536,2048]{1,0:T(8,128)} %fusion.47, f32[1536,2048]{1,0:T(8,128)} %get-tuple-element.329, bf16[1536,2048]{1,0:T(8,128)(2,1)} %get-tuple-element.303, bf16[2048,2048]{1,0:T(8,128)(2,1)} %all-gather.21.cloned.1.call-done), kind=kOutput, calls=%fused_computation.48 | convolution fusion | flops 12925796352 | bytes 52428800 | tf_op jit(solution)/shard_map/dot_general | solution.py:32
  1124.0 19.2 fusion.49
  1143.2 20.6 convolution_add_fusion
  1168.3 234.9 %all-reduce.11.cloned.1.call-done = f32[1536,2048]{1,0:T(8,128)} async-done(((f32[1536,2048]{1,0:T(8,128)}), f32[1536,2048]{1,0:T(8,128)}) %all-reduce.11.cloned.1.call-update) | async-done | bytes 12582928 | tf_op jit(solution)/shard_map/psum | solution.py:265
  1403.3 12.4 multiply_reduce_fusion.1
  1415.7 10.6 subtract_convert_fusion
  1426.4 4.6 convolution_convert_fusion.7
  1431.0 119.3 %while.30 = (s32[]{:T(128)}, f32[1536,4,128]{0,2,1:T(8,128)}, f32[1536,4,128]{0,2,1:T(8,128)}, f32[3,512,512]{2,1,0:T(8,128)}, bf16[3,512,512]{1,2,0:T(8,128)(2,...) while((s32[]{:T(128)}, f32[1536,4,128]{0,2,1:T(8,128)}, ...), condition=%wide.region_17.18_spmd.clone.clone, body=%wide.region_15.17_spmd.clone.sunk.clone | while | flops 4062182912 | bytes 262219120 | solution.py:177
  1440.0 6.2 multiply_reduce_fusion.11
  1452.7 5.8 fusion.155
  1477.8 6.2 multiply_reduce_fusion.11
  1490.4 6.7 fusion.155
  1499.0 4.9 fusion.156
  1518.3 6.2 multiply_reduce_fusion.11
  1531.0 6.7 fusion.155
  1539.5 4.9 fusion.156
  1553.5 4.9 reshape_reshape.3
  1558.4 9.5 multiply_subtract_fusion
  1570.8 5.0 copy.51
  1582.6 5.1 copy.54
  1590.3 15.1 all-reduce.1
  1610.3 7.6 convolution_convert_fusion.6
  1621.8 7.9 convolution_convert_fusion.5
  1631.3 8.0 convolution_convert_fusion.4
  1639.4 7.5 convolution_convert_fusion.3
  1647.0 19.4 convolution_convert_fusion.2
  1666.4 19.6 convolution_convert_fusion.1
  1686.2 19.9 convolution_convert_fusion
  1707.5 8.5 fusion.50
  1716.0 6.4 fusion.51
  1722.5 13.2 add_convert_fusion
  1737.3 4.8 fusion.23
  1743.5 40.2 %all-reduce = (f32[2048]{0:T(1024)S(1)}, f32[2048]{0:T(1024)S(1)}, f32[2048]{0:T(1024)}, f32[2048]{0:T(1024)}) all-reduce(f32[2048]{0:T(1024)S(1)} %dynamic_update_slice.23, f32[2048]{0:T(1024)S(1)} %dynamic_update_slice.24, f32[2048]{0:T(1024)S(1)} %dynamic-slice_dynamic-update-slice_fusion.1, ...), channel_id=1, replica_groups=mesh['row'=8,'col'=4] {'row','col'}, use_global_device_ids=true, to_apply=%region_31.32 | all-reduce | flops 8192 | bytes 65536 | tf_op jit(solution)/shard_map/psum | solution.py:332
  1792.2 64.3 %reduce-scatter.19.cloned.1.call-done = bf16[256,2048]{1,0:T(8,128)(2,1)} async-done(((bf16[2048,2048]{1,0:T(8,128)(2,1)}), bf16[256,2048]{1,0:T(8,128)(2,1)}) %reduce-scatter.19.cloned.1.call-update) | async-done | bytes 1048592 | tf_op jit(solution)/shard_map/reduce_scatter | solution.py:322
  1859.3 87.4 %reduce-scatter.21.cloned.1.call-done = bf16[256,2048]{1,0:T(8,128)(2,1)} async-done(((bf16[2048,2048]{1,0:T(8,128)(2,1)}), bf16[256,2048]{1,0:T(8,128)(2,1)}) %reduce-scatter.21.cloned.1.call-update) | async-done | bytes 1048592 | tf_op jit(solution)/shard_map/reduce_scatter | solution.py:325
  1949.4 87.4 %reduce-scatter.23.cloned.1.call-done = bf16[2048,256]{1,0:T(8,128)(2,1)} async-done(((bf16[2048,2048]{1,0:T(8,128)(2,1)}), bf16[2048,256]{1,0:T(8,128)(2,1)}) %reduce-scatter.23.cloned.1.call-update) | async-done | bytes 1048592 | tf_op jit(solution)/shard_map/reduce_scatter | solution.py:328
  2039.5 68.8 %reduce-scatter.9.cloned.1.call-done = bf16[1536,512]{1,0:T(8,128)(2,1)} async-done(((bf16[1536,2048]{1,0:T(8,128)(2,1)}), bf16[1536,512]{1,0:T(8,128)(2,1)}) %reduce-scatter.9.cloned.1.call-update) | async-done | bytes 1572880 | tf_op jit(solution)/shard_map/reduce_scatter | solution.py:304
  (329 shorter events, 226.7 us)
Async XLA Ops:
  7.2 119.0 %all-gather.11.cloned.1.call-start = ((), (), s32[]{:S(2)}) async-start(), calls=%async_computation.9 | async-start | bytes 2359296 | tf_op jit(solution)/shard_map/all_gather | solution.py:207
  7.9 124.6 %all-gather.9.cloned.1.call-start = ((), (), s32[]{:S(2)}) async-start(), calls=%async_computation.8 | async-start | bytes 2359296 | tf_op jit(solution)/shard_map/all_gather | solution.py:206
  8.7 186.8 %all-gather.13.cloned.1.call-start = ((), (), s32[]{:S(2)}) async-start(), calls=%async_computation.10 | async-start | bytes 2359296 | tf_op jit(solution)/shard_map/all_gather | solution.py:208
  9.4 241.9 %all-gather.15.cloned.1.call-start = ((), (), s32[]{:S(2)}) async-start(), calls=%async_computation.11 | async-start | bytes 2359296 | tf_op jit(solution)/shard_map/all_gather | solution.py:209
  9.4 38.6 %collective-permute-start = (bf16[1536,512]{1,0:T(8,128)(2,1)}, bf16[1536,512]{1,0:T(8,128)(2,1)S(1)}, u32[]{:S(2)}, u32[]{:S(2)}) collective-permute-start(bf16[1536,512]{1,0:T(8,128)(2,1)} %param.19), channel_id=1, source_target_pairs={{0,1},{1,2},{2,3},{3,0},{4,5},{5,6},{6,7},{7,4},{8,9},{9,10},{10,1... | collective-permute-start | bytes 4718600 | tf_op jit(solution)/shard_map/ppermute | solution.py:20
  48.0 38.3 %collective-permute-start.1 = (bf16[1536,512]{1,0:T(8,128)(2,1)S(1)}, bf16[1536,512]{1,0:T(8,128)(2,1)}, u32[]{:S(2)}, u32[]{:S(2)}) collective-permute-start(bf16[1536,512]{1,0:T(8,128)(2,1)S(1)} %collective-permute-done), channel_id=1, source_target_pairs={{0,1},{1,2},{2,3},{3,0},{4,5},{5,6},{6,7},{7,4},{8,9},{9,10},{10,1... | collective-permute-start | bytes 4718600 | tf_op jit(solution)/shard_map/ppermute | solution.py:20
  48.8 69.3 %collective-permute-start.2 = (bf16[1536,512]{1,0:T(8,128)(2,1)}, bf16[1536,512]{1,0:T(8,128)(2,1)S(1)}, u32[]{:S(2)}, u32[]{:S(2)}) collective-permute-start(bf16[1536,512]{1,0:T(8,128)(2,1)} %param.19), channel_id=1, source_target_pairs={{0,3},{1,0},{2,1},{3,2},{4,7},{5,4},{6,5},{7,6},{8,11},{9,8},{10,9... | collective-permute-start | bytes 4718600 | tf_op jit(solution)/shard_map/ppermute | solution.py:22
  51.0 450.2 %all-reduce.7.cloned.1.call-start = ((), (), s32[]{:S(2)}) async-start(), calls=%async_computation.12 | async-start | bytes 25165824 | tf_op jit(solution)/shard_map/psum | solution.py:232
  58.8 31.5 %copy-start.21 = (bf16[1536,512]{1,0:T(8,128)(2,1)S(1)}, bf16[1536,512]{1,0:T(8,128)(2,1)}, u32[]{:S(2)}) copy-start(bf16[1536,512]{1,0:T(8,128)(2,1)} %param.19) | copy-start | bytes 4718596
  132.4 24.3 %copy-start.10 = (f32[1536,512]{0,1:T(8,128)}, f32[1536,512]{0,1:T(8,128)S(1)}, u32[]{:S(2)}) copy-start(f32[1536,512]{0,1:T(8,128)S(1)} %get-tuple-element.327) | copy-start | bytes 9437188
  132.5 24.3 %copy-start.50 = (f32[512]{0:T(512)S(1)}, f32[512]{0:T(512)}, u32[]{:S(2)}) copy-start(f32[512]{0:T(512)} %param.28) | copy-start | bytes 6148
  156.7 9.0 copy-start.39
  185.5 6.4 copy-start.22
  185.5 6.4 copy-start.23
  195.4 8.1 copy-start.25
  195.4 8.1 copy-start.35
  251.3 10.1 copy-start.43
  251.3 10.1 copy-start.44
  261.5 323.3 %all-gather.17.cloned.1.call-start = ((), (), s32[]{:S(2)}) async-start(), calls=%async_computation.13 | async-start | bytes 9437184 | tf_op jit(solution)/shard_map/all_gather | solution.py:210
  262.0 404.8 %all-gather.19.cloned.1.call-start = ((), (), s32[]{:S(2)}) async-start(), calls=%async_computation.14 | async-start | bytes 9437184 | tf_op jit(solution)/shard_map/all_gather | solution.py:211
  262.8 486.7 %all-gather.21.cloned.1.call-start = ((), (), s32[]{:S(2)}) async-start(), calls=%async_computation.15 | async-start | bytes 9437184 | tf_op jit(solution)/shard_map/all_gather | solution.py:212
  263.5 243.9 %copy-start.45 = (f32[2048]{0:T(1024)S(1)}, f32[2048]{0:T(1024)}, u32[]{:S(2)}) copy-start(f32[2048]{0:T(1024)} %param.29) | copy-start | bytes 24580
  263.6 742.5 %all-reduce.9.cloned.1.call-start = ((), (), s32[]{:S(2)}) async-start(), calls=%async_computation.16 | async-start | bytes 25165824 | tf_op jit(solution)/shard_map/psum | solution.py:244
  501.2 8.3 copy-start.2
  768.4 309.2 %all-gather.23.cloned.1.call-start = ((), (), s32[]{:S(2)}) async-start(), calls=%async_computation.17 | async-start | bytes 7864320 | tf_op jit(solution)/shard_map/all_gather | solution.py:250
  769.0 308.6 %copy-start.47 = (f32[2048]{0:T(1024)S(1)}, f32[2048]{0:T(1024)}, u32[]{:S(2)}) copy-start(f32[2048]{0:T(1024)} %param.30) | copy-start | bytes 24580
  769.0 634.3 %all-reduce.11.cloned.1.call-start = ((), (), s32[]{:S(2)}) async-start(), calls=%async_computation.18 | async-start | bytes 25165824 | tf_op jit(solution)/shard_map/psum | solution.py:265
  1077.6 10.3 copy-start.5
  1077.6 11.8 copy-start.9
  1124.0 19.2 copy-start.54
  1163.8 621.1 %reduce-scatter.11.cloned.1.call-start = ((), (), s32[]{:S(2)}) async-start(), calls=%async_computation.20 | async-start | bytes 2359296 | tf_op jit(solution)/shard_map/reduce_scatter | solution.py:310
  1165.2 238.1 %copy-start.42 = (f32[1536]{0:T(1024)S(1)}, f32[1536]{0:T(1024)}, u32[]{:S(2)}) copy-start(f32[1536]{0:T(1024)} %copy-done.41) | copy-start | bytes 18436
  1165.2 238.1 %copy-start.46 = (f32[2048]{0:T(1024)S(1)}, f32[2048]{0:T(1024)}, u32[]{:S(2)}) copy-start(f32[2048]{0:T(1024)} %param.29) | copy-start | bytes 24580
  1415.7 10.6 copy-start.7
  1415.7 10.6 copy-start.53
  1431.4 5.4 copy-start.3
  1446.3 6.4 copy-start
  1452.7 7.7 copy-start.1
  1452.7 10.4 slice-start
  1469.2 5.4 copy-start.3
  1484.0 6.4 copy-start
  1490.4 8.6 copy-start.1
  1490.4 13.4 slice-start
  1509.7 5.4 copy-start.3
  1524.6 6.4 copy-start
  1531.0 8.6 copy-start.1
  1531.0 13.4 slice-start
  1570.8 5.1 copy-start.49
  1582.6 5.1 copy-start.11
  1582.6 5.1 copy-start.38
  1582.6 5.1 copy-start.51
  1617.9 168.9 %reduce-scatter.13.cloned.1.call-start = ((), (), s32[]{:S(2)}) async-start(), calls=%async_computation.21 | async-start | bytes 2359296 | tf_op jit(solution)/shard_map/reduce_scatter | solution.py:313
  1621.8 8.0 copy-start.6
  1629.8 158.8 %reduce-scatter.15.cloned.1.call-start = ((), (), s32[]{:S(2)}) async-start(), calls=%async_computation.22 | async-start | bytes 2359296 | tf_op jit(solution)/shard_map/reduce_scatter | solution.py:316
  1631.3 8.1 copy-start.30
  1639.3 151.1 %reduce-scatter.17.cloned.1.call-start = ((), (), s32[]{:S(2)}) async-start(), calls=%async_computation.23 | async-start | bytes 2359296 | tf_op jit(solution)/shard_map/reduce_scatter | solution.py:319
  1646.9 209.6 %reduce-scatter.19.cloned.1.call-start = ((), (), s32[]{:S(2)}) async-start(), calls=%async_computation.24 | async-start | bytes 9437184 | tf_op jit(solution)/shard_map/reduce_scatter | solution.py:322
  1666.4 280.3 %reduce-scatter.21.cloned.1.call-start = ((), (), s32[]{:S(2)}) async-start(), calls=%async_computation.25 | async-start | bytes 9437184 | tf_op jit(solution)/shard_map/reduce_scatter | solution.py:325
  1686.1 350.7 %reduce-scatter.23.cloned.1.call-start = ((), (), s32[]{:S(2)}) async-start(), calls=%async_computation.26 | async-start | bytes 9437184 | tf_op jit(solution)/shard_map/reduce_scatter | solution.py:328
  1706.1 402.2 %reduce-scatter.9.cloned.1.call-start = ((), (), s32[]{:S(2)}) async-start(), calls=%async_computation.19 | async-start | bytes 7864320 | tf_op jit(solution)/shard_map/reduce_scatter | solution.py:304
  1707.5 8.5 copy-start.34
  1707.5 8.5 copy-start.52
  1716.0 6.5 copy-start.20
  1716.0 6.5 copy-start.27
  (31 other events, 100.4 us)
Sparse Core Ops, SparseCore 0:
  9.6 31.8 all-gather.10
  43.1 28.5 all-gather.8
  73.3 28.5 all-gather.12
  103.3 29.9 all-gather.14
  261.6 239.5 all-reduce.6
  502.7 82.0 all-gather.16
  586.3 80.5 all-gather.18
  668.5 80.9 all-gather.20
  768.5 237.4 all-reduce.8
  1007.7 69.8 all-gather.22
  1164.0 239.2 all-reduce.10
  1618.0 36.0 reduce-scatter.10
  1657.0 34.5 reduce-scatter.12
  1694.3 34.5 reduce-scatter.14
  1731.6 34.7 reduce-scatter.16
  1768.6 87.8 reduce-scatter.18
  1858.6 87.9 reduce-scatter.20
  1948.8 87.9 reduce-scatter.22
  2039.8 68.4 reduce-scatter.8
